TPU v7x, 32 devices: a whole 2x2x4 slice. The times are simulated.
32 devices in a mesh: dp: 8 (over y, x, core), mp: 4 (over z).
Axes of the slice: x: 2, y: 2, z: 4, core: 2. Of those that a mesh axis runs over, the one named last changes fastest.
Arguments:
- layer_input: bfloat16 [32, 8192], P('dp'), may hold values from -6 to 6
- pre_act: bfloat16 [32, 8192], P('dp', 'mp'), may hold values from -8 to 8
- hidden_adjoint: bfloat16 [32, 8192], P('dp', 'mp'), may hold values from -6 to 6
- output_adjoint: bfloat16 [32, 8192], P('dp', 'mp'), may hold values from -6 to 6
Outputs:
- precond_in: float32 [8192, 8192], P('dp', 'mp')
- direction_in: float32 [8192, 8192], P('dp', 'mp')
- precond_out: float32 [8192, 8192], P('dp', 'mp')
- direction_out: float32 [8192, 8192], P('dp', 'mp')
- sq_norm: float32 [], replicated
All inputs are finite; a program needn't handle non-finite values.
Results may differ from a plain program's by a relative error of at most 0.0029.
Values may be sent and summed in bfloat16 or wider, within the bound.
A program may use at most 64 MiB of HBM per device.

v0:
```python
import jax
import jax.numpy as jnp
from jax import lax
from jax.sharding import PartitionSpec as P

D = 8192
H = 8192
DAMPING = 0.1
EXPONENT = 0.75


def square_bf(values):
    wide = values.astype(jnp.float32)
    return (wide * wide).astype(jnp.bfloat16)


def accumulate(act_block, sq_block, adj_piece):
    contract = (((0,), (0,)), ((), ()))
    grad_sum = lax.dot_general(act_block, adj_piece, contract, preferred_element_type=jnp.float32)
    square_sum = lax.dot_general(
        sq_block, square_bf(adj_piece), contract, preferred_element_type=jnp.float32
    )
    return (grad_sum, square_sum)


def finish(partial_value, total_rows):
    gradient = partial_value[0] / total_rows
    precond = (partial_value[1] / total_rows + DAMPING) ** EXPONENT
    norm_term = jnp.sum(gradient * gradient / precond)
    return (gradient, precond, norm_term)


def shards(layer_input, pre_act, hidden_adjoint, output_adjoint):
    preact = pre_act.astype(jnp.float32)
    logistic = jax.nn.sigmoid(preact)
    hidden = (preact * logistic).astype(jnp.bfloat16)
    adjoint = (
        hidden_adjoint.astype(jnp.float32) * logistic * (1.0 + preact * (1.0 - logistic))
    ).astype(jnp.bfloat16)
    own_input = lax.all_to_all(layer_input, "dp", split_axis=1, concat_axis=0, tiled=True)
    sq_input = square_bf(own_input)
    total_rows = own_input.shape[0]
    wide_hidden = lax.all_gather(hidden, "mp", axis=1, tiled=True)
    own_hidden = lax.all_to_all(wide_hidden, "dp", split_axis=1, concat_axis=0, tiled=True)
    sq_hidden = square_bf(own_hidden)
    sums_in = accumulate(own_input, sq_input, lax.all_gather(adjoint, "dp", axis=0, tiled=True))
    sums_out = accumulate(
        own_hidden, sq_hidden, lax.all_gather(output_adjoint, "dp", axis=0, tiled=True)
    )
    gradient_in, precond_in, term_in = finish(sums_in, total_rows)
    gradient_out, precond_out, term_out = finish(sums_out, total_rows)
    sq_norm = lax.psum(term_in + term_out, ("dp", "mp"))
    rescale = jnp.sqrt(2.0 * D * H / sq_norm)
    direction_in = gradient_in / precond_in * rescale
    direction_out = gradient_out / precond_out * rescale
    return (precond_in, direction_in, precond_out, direction_out, sq_norm)


def solution(mesh):
    placed = (P("dp", None), P("dp", "mp"), P("dp", "mp"), P("dp", "mp"))
    return jax.shard_map(
        shards,
        mesh=mesh,
        in_specs=placed,
        out_specs=(P("dp", "mp"), P("dp", "mp"), P("dp", "mp"), P("dp", "mp"), P()),
        check_vma=False,
    )
```

profile of v0, /device:TPU:0, one launch (start us, length us, event | category | flops | bytes accessed | tf_op | source)
XLA Modules:
  0.0 133.4 jit_solution(15350232104087235126)
XLA Ops:
  0.6 5.2 %all-to-all-start = ((bf16[4,8,1024]{2,0,1:T(4,128)(2,1)}), bf16[4,8,1024]{2,0,1:T(4,128)(2,1)S(1)}, u32[]{:S(2)}, u32[]{:S(2)}) async-start(bf16[4,8,1024]{2,0,1:T(4,128)(2,1)} %bitcast.22), calls=%async_computation | async-start | bytes 131072 | tf_op jit(solution)/shard_map/all_to_all | solution.py:40
  5.8 0.8 fusion.13
  6.6 14.1 %all_gather.10 = bf16[4,8192]{1,0:T(4,128)(2,1)} all-gather(bf16[4,2048]{1,0:T(4,128)(2,1)S(1)} %get-tuple-element.9), channel_id=1, replica_groups=mesh['dp'=8,'mp'=4] {'mp'}, dimensions={1}, use_global_device_ids=true | all-gather | bytes 81920 | tf_op jit(solution)/shard_map/all_gather | solution.py:43
  20.7 0.0 all-to-all-done
  20.7 4.3 %all-to-all-start.1 = ((bf16[4,8,1024]{2,0,1:T(4,128)(2,1)}), bf16[4,8,1024]{2,0,1:T(4,128)(2,1)S(1)}, u32[]{:S(2)}, u32[]{:S(2)}) async-start(bf16[4,8,1024]{2,0,1:T(4,128)(2,1)} %bitcast.4), calls=%async_computation.1 | async-start | bytes 131072 | tf_op jit(solution)/shard_map/all_to_all | solution.py:44
  25.0 9.7 %all-gather = bf16[8,4,2048]{2,1,0:T(4,128)(2,1)S(1)} all-gather(bf16[1,4,2048]{2,1,0:T(4,128)(2,1)S(1)} %get-tuple-element.10), channel_id=1, replica_groups=mesh['dp'=8,'mp'=4] {'dp'}, dimensions={0}, use_global_device_ids=true | all-gather | bytes 147456 | tf_op jit(solution)/shard_map/all_gather | solution.py:46
  34.7 9.2 %all-gather.1 = bf16[8,4,2048]{2,1,0:T(4,128)(2,1)S(1)} all-gather(bf16[1,4,2048]{2,1,0:T(4,128)(2,1)} %bitcast.23), channel_id=1, replica_groups=mesh['dp'=8,'mp'=4] {'dp'}, dimensions={0}, use_global_device_ids=true | all-gather | bytes 147456 | tf_op jit(solution)/shard_map/all_gather | solution.py:48
  44.0 0.0 all-to-all-done.1
  44.0 1.3 fusion.6
  45.3 0.0 copy-start
  45.3 7.8 %multiply_reduce_fusion = (f32[]{:T(128)}, f32[1024,2048]{1,0:T(8,128)}) fusion(f32[1024,2048]{1,0:T(8,128)S(1)} %fusion.6, bf16[32,1024]{1,0:T(8,128)(2,1)S(1)} %all_to_all.35, bf16[32,2048]{1,0:T(8,128)(2,1)S(1)} %reshape.19), kind=kOutput, calls=%fused_computation.6 | convolution fusion | flops 146800640 | bytes 16973828 | tf_op jit(solution)/shard_map/dot_general | solution.py:19
  53.1 0.0 copy-done
  53.1 1.3 fusion.5
  54.3 0.0 copy-start.1
  54.4 7.7 %fusion.2 = (f32[]{:T(128)}, f32[2048,1024]{0,1:T(8,128)}) fusion(f32[1024,2048]{1,0:T(8,128)S(1)} %fusion.5, bf16[32,2048]{1,0:T(8,128)(2,1)S(1)} %reshape.17, bf16[32,1024]{1,0:T(8,128)(2,1)S(1)} %all_to_all.31), kind=kOutput, calls=%fused_computation.4 | convolution fusion | flops 146800640 | bytes 16973828 | tf_op jit(solution)/shard_map/dot_general | solution.py:19
  62.0 0.0 copy-done.1
  63.3 39.4 %psum.7 = f32[]{:T(128)} all-reduce(f32[]{:T(128)S(6)} %add.21), channel_id=1, replica_groups=mesh['dp'=8,'mp'=4] {'dp','mp'}, use_global_device_ids=true, to_apply=%region_2.0 | all-reduce | flops 1 | bytes 8 | tf_op jit(solution)/shard_map/psum | solution.py:52
  103.5 29.9 %fusion = (f32[1024,2048]{1,0:T(8,128)}, f32[1024,2048]{1,0:T(8,128)}, f32[1024,2048]{1,0:T(8,128)}, f32[1024,2048]{1,0:T(8,128)}) fusion(f32[2048,1024]{0,1:T(8,128)} %get-tuple-element.12, f32[1024,2048]{1,0:T(8,128)} %copy-done.1, f32[]{:T(128)S(6)} %sqrt.3, f32[1024,2048]{1,0:T(8,128)} %copy-done, f32[1024,2048]{1,0:T(8,128)} %get-tuple-element.14), kind=kLoop, calls=%fused_computation.2 | loop fusion | flops 20971520 | bytes 67108864 | tf_op jit(solution)/shard_map/mul | solution.py:54
  (4 shorter events, 0.1 us)
Async XLA Ops:
  0.6 20.1 %all-to-all-start = ((bf16[4,8,1024]{2,0,1:T(4,128)(2,1)}), bf16[4,8,1024]{2,0,1:T(4,128)(2,1)S(1)}, u32[]{:S(2)}, u32[]{:S(2)}) async-start(bf16[4,8,1024]{2,0,1:T(4,128)(2,1)} %bitcast.22), calls=%async_computation | async-start | bytes 131072 | tf_op jit(solution)/shard_map/all_to_all | solution.py:40
  20.7 23.2 %all-to-all-start.1 = ((bf16[4,8,1024]{2,0,1:T(4,128)(2,1)}), bf16[4,8,1024]{2,0,1:T(4,128)(2,1)S(1)}, u32[]{:S(2)}, u32[]{:S(2)}) async-start(bf16[4,8,1024]{2,0,1:T(4,128)(2,1)} %bitcast.4), calls=%async_computation.1 | async-start | bytes 131072 | tf_op jit(solution)/shard_map/all_to_all | solution.py:44
  45.3 7.8 %copy-start = (f32[1024,2048]{1,0:T(8,128)}, f32[1024,2048]{1,0:T(8,128)S(1)}, u32[]{:S(2)}) copy-start(f32[1024,2048]{1,0:T(8,128)S(1)} %fusion.6) | copy-start | bytes 25165828
  54.3 7.7 %copy-start.1 = (f32[1024,2048]{1,0:T(8,128)}, f32[1024,2048]{1,0:T(8,128)S(1)}, u32[]{:S(2)}) copy-start(f32[1024,2048]{1,0:T(8,128)S(1)} %fusion.5) | copy-start | bytes 25165828
where the time goes:
time: 134 us; the launch traced here: 133 us
  blocking collectives  72.4 us (54%)
  other arithmetic  30.6 us (23%)
  matrix products  18 us (13%)
  starting transfers between devices  9.48 us (7%)
  between operations  2.7 us (2%)
    psum x1, blocking collectives, shards(): sq_norm = lax.psum(term_in + term_out, ('dp', 'mp'))  39.4 us
    mul x1, other arithmetic, shards(): direction_in = gradient_in / precond_in * rescale  29.9 us
    dot_general x2, matrix products, accumulate(): lax.dot_general(act_block, adj_piece, contract, preferred_element_type=jn...  15.4 us
    all_gather x1, blocking collectives, shards(): wide_hidden = lax.all_gather(hidden, 'mp', axis=1, tiled=True)  14.1 us
    all_gather x1, blocking collectives, shards(): lax.all_gather(adjoint, 'dp', axis=0, tiled=True)  9.71 us
    all_gather x1, blocking collectives, shards(): lax.all_gather(output_adjoint, 'dp', axis=0, tiled=True)  9.16 us
    all_to_all x1, starting transfers between devices, shards(): lax.all_to_all(layer_input, 'dp', split_axis=1, concat_axis=0, tiled=True)  5.21 us
    all_to_all x1, starting transfers between devices, shards(): lax.all_to_all(wide_hidden, 'dp', split_axis=1, concat_axis=0, tiled=True)  4.27 us
  transfers between devices with their start and end apart: 2, of which 0 were waited for; matrix products, arithmetic and copies ran while one was open for 1% of the time, Pallas kernels for 0%

commit v1 on v0

--- a/solution.py
+++ b/solution.py
@@ -49,7 +49,7 @@
     )
     gradient_in, precond_in, term_in = finish(sums_in, total_rows)
     gradient_out, precond_out, term_out = finish(sums_out, total_rows)
-    sq_norm = lax.psum(term_in + term_out, ("dp", "mp"))
+    sq_norm = lax.psum(lax.psum(term_in + term_out, "mp"), "dp")
     rescale = jnp.sqrt(2.0 * D * H / sq_norm)
     direction_in = gradient_in / precond_in * rescale
     direction_out = gradient_out / precond_out * rescale

time: 134 us -> 119 us (0.89)
  blocking collectives: 72.4 us -> 57.7 us
    psum x1 -> x2, blocking collectives: 39.4 us -> 24.8 us  [shards(): sq_norm = lax.psum(lax.psum(term_in + term_out, 'mp'), 'dp')]
where the time goes in v1:
time: 119 us
  blocking collectives  57.7 us (48%)
  other arithmetic  30.6 us (26%)
  matrix products  18 us (15%)
  starting transfers between devices  9.48 us (8%)
  between operations  2.75 us (2%)
    mul x1, other arithmetic, shards(): direction_in = gradient_in / precond_in * rescale  29.9 us
    psum x2, blocking collectives, shards(): sq_norm = lax.psum(lax.psum(term_in + term_out, 'mp'), 'dp')  24.8 us
    dot_general x2, matrix products, accumulate(): lax.dot_general(act_block, adj_piece, contract, preferred_element_type=jn...  15.5 us
    all_gather x1, blocking collectives, shards(): wide_hidden = lax.all_gather(hidden, 'mp', axis=1, tiled=True)  14.1 us
    all_gather x1, blocking collectives, shards(): lax.all_gather(adjoint, 'dp', axis=0, tiled=True)  9.71 us
    all_gather x1, blocking collectives, shards(): lax.all_gather(output_adjoint, 'dp', axis=0, tiled=True)  9.16 us
    all_to_all x1, starting transfers between devices, shards(): lax.all_to_all(layer_input, 'dp', split_axis=1, concat_axis=0, tiled=True)  5.21 us
    all_to_all x1, starting transfers between devices, shards(): lax.all_to_all(wide_hidden, 'dp', split_axis=1, concat_axis=0, tiled=True)  4.27 us
  transfers between devices with their start and end apart: 2, of which 0 were waited for; matrix products, arithmetic and copies ran while one was open for 1% of the time, Pallas kernels for 0%

profile of v1, /device:TPU:0, one launch (start us, length us, event | category | flops | bytes accessed | tf_op | source)
XLA Modules:
  0.0 118.8 jit_solution(18145692517896413084)
XLA Ops:
  0.6 5.2 %all-to-all-start = ((bf16[4,8,1024]{2,0,1:T(4,128)(2,1)}), bf16[4,8,1024]{2,0,1:T(4,128)(2,1)S(1)}, u32[]{:S(2)}, u32[]{:S(2)}) async-start(bf16[4,8,1024]{2,0,1:T(4,128)(2,1)} %bitcast.22), calls=%async_computation | async-start | bytes 131072 | tf_op jit(solution)/shard_map/all_to_all | solution.py:40
  5.8 0.8 fusion.13
  6.6 14.1 %all_gather.10 = bf16[4,8192]{1,0:T(4,128)(2,1)} all-gather(bf16[4,2048]{1,0:T(4,128)(2,1)S(1)} %get-tuple-element.9), channel_id=1, replica_groups=mesh['dp'=8,'mp'=4] {'mp'}, dimensions={1}, use_global_device_ids=true | all-gather | bytes 81920 | tf_op jit(solution)/shard_map/all_gather | solution.py:43
  20.7 0.0 all-to-all-done
  20.7 4.3 %all-to-all-start.1 = ((bf16[4,8,1024]{2,0,1:T(4,128)(2,1)}), bf16[4,8,1024]{2,0,1:T(4,128)(2,1)S(1)}, u32[]{:S(2)}, u32[]{:S(2)}) async-start(bf16[4,8,1024]{2,0,1:T(4,128)(2,1)} %bitcast.4), calls=%async_computation.1 | async-start | bytes 131072 | tf_op jit(solution)/shard_map/all_to_all | solution.py:44
  25.0 9.7 %all-gather = bf16[8,4,2048]{2,1,0:T(4,128)(2,1)S(1)} all-gather(bf16[1,4,2048]{2,1,0:T(4,128)(2,1)S(1)} %get-tuple-element.10), channel_id=1, replica_groups=mesh['dp'=8,'mp'=4] {'dp'}, dimensions={0}, use_global_device_ids=true | all-gather | bytes 147456 | tf_op jit(solution)/shard_map/all_gather | solution.py:46
  34.7 9.2 %all-gather.1 = bf16[8,4,2048]{2,1,0:T(4,128)(2,1)S(1)} all-gather(bf16[1,4,2048]{2,1,0:T(4,128)(2,1)} %bitcast.23), channel_id=1, replica_groups=mesh['dp'=8,'mp'=4] {'dp'}, dimensions={0}, use_global_device_ids=true | all-gather | bytes 147456 | tf_op jit(solution)/shard_map/all_gather | solution.py:48
  44.0 0.0 all-to-all-done.1
  44.0 1.3 %fusion.6 = f32[1024,2048]{1,0:T(8,128)S(1)} fusion(bf16[32,2048]{1,0:T(8,128)(2,1)S(1)} %reshape.19, bf16[32,1024]{1,0:T(8,128)(2,1)S(1)} %all_to_all.35), kind=kOutput, calls=%fused_computation.14 | convolution fusion | flops 134512640 | bytes 8585216 | tf_op jit(solution)/shard_map/dot_general | solution.py:20
  45.3 0.0 copy-start
  45.3 7.8 %multiply_reduce_fusion = (f32[]{:T(128)}, f32[1024,2048]{1,0:T(8,128)}) fusion(f32[1024,2048]{1,0:T(8,128)S(1)} %fusion.6, bf16[32,1024]{1,0:T(8,128)(2,1)S(1)} %all_to_all.35, bf16[32,2048]{1,0:T(8,128)(2,1)S(1)} %reshape.19), kind=kOutput, calls=%fused_computation.6 | convolution fusion | flops 146800640 | bytes 16973828 | tf_op jit(solution)/shard_map/dot_general | solution.py:19
  53.1 0.0 copy-done
  53.1 1.3 %fusion.5 = f32[1024,2048]{1,0:T(8,128)S(1)} fusion(bf16[32,2048]{1,0:T(8,128)(2,1)S(1)} %reshape.17, bf16[32,1024]{1,0:T(8,128)(2,1)S(1)} %all_to_all.31), kind=kOutput, calls=%fused_computation.13 | convolution fusion | flops 134512640 | bytes 8585216 | tf_op jit(solution)/shard_map/dot_general | solution.py:20
  54.4 0.0 copy-start.1
  54.4 7.7 %fusion.2 = (f32[]{:T(128)}, f32[2048,1024]{0,1:T(8,128)}) fusion(f32[1024,2048]{1,0:T(8,128)S(1)} %fusion.5, bf16[32,2048]{1,0:T(8,128)(2,1)S(1)} %reshape.17, bf16[32,1024]{1,0:T(8,128)(2,1)S(1)} %all_to_all.31), kind=kOutput, calls=%fused_computation.4 | convolution fusion | flops 146800640 | bytes 16973828 | tf_op jit(solution)/shard_map/dot_general | solution.py:19
  62.1 0.0 copy-done.1
  63.4 12.2 %psum.14 = f32[]{:T(128)} all-reduce(f32[]{:T(128)S(6)} %add.23), channel_id=1, replica_groups=mesh['dp'=8,'mp'=4] {'mp'}, use_global_device_ids=true, to_apply=%region_2.0 | all-reduce | flops 1 | bytes 8 | tf_op jit(solution)/shard_map/psum | solution.py:52
  75.6 12.6 %psum.15 = f32[]{:T(128)} all-reduce(f32[]{:T(128)} %psum.14), channel_id=1, replica_groups=mesh['dp'=8,'mp'=4] {'dp'}, use_global_device_ids=true, to_apply=%region_3.0 | all-reduce | flops 1 | bytes 8 | tf_op jit(solution)/shard_map/psum | solution.py:52
  88.9 29.9 %fusion = (f32[1024,2048]{1,0:T(8,128)}, f32[1024,2048]{1,0:T(8,128)}, f32[1024,2048]{1,0:T(8,128)}, f32[1024,2048]{1,0:T(8,128)}) fusion(f32[2048,1024]{0,1:T(8,128)} %get-tuple-element.12, f32[1024,2048]{1,0:T(8,128)} %copy-done.1, f32[]{:T(128)S(6)} %sqrt.3, f32[1024,2048]{1,0:T(8,128)} %copy-done, f32[1024,2048]{1,0:T(8,128)} %get-tuple-element.14), kind=kLoop, calls=%fused_computation.2 | loop fusion | flops 20971520 | bytes 67108864 | tf_op jit(solution)/shard_map/mul | solution.py:54
  (4 shorter events, 0.1 us)
Async XLA Ops:
  0.6 20.1 %all-to-all-start = ((bf16[4,8,1024]{2,0,1:T(4,128)(2,1)}), bf16[4,8,1024]{2,0,1:T(4,128)(2,1)S(1)}, u32[]{:S(2)}, u32[]{:S(2)}) async-start(bf16[4,8,1024]{2,0,1:T(4,128)(2,1)} %bitcast.22), calls=%async_computation | async-start | bytes 131072 | tf_op jit(solution)/shard_map/all_to_all | solution.py:40
  20.7 23.2 %all-to-all-start.1 = ((bf16[4,8,1024]{2,0,1:T(4,128)(2,1)}), bf16[4,8,1024]{2,0,1:T(4,128)(2,1)S(1)}, u32[]{:S(2)}, u32[]{:S(2)}) async-start(bf16[4,8,1024]{2,0,1:T(4,128)(2,1)} %bitcast.4), calls=%async_computation.1 | async-start | bytes 131072 | tf_op jit(solution)/shard_map/all_to_all | solution.py:44
  45.3 7.8 %copy-start = (f32[1024,2048]{1,0:T(8,128)}, f32[1024,2048]{1,0:T(8,128)S(1)}, u32[]{:S(2)}) copy-start(f32[1024,2048]{1,0:T(8,128)S(1)} %fusion.6) | copy-start | bytes 25165828
  54.4 7.7 %copy-start.1 = (f32[1024,2048]{1,0:T(8,128)}, f32[1024,2048]{1,0:T(8,128)S(1)}, u32[]{:S(2)}) copy-start(f32[1024,2048]{1,0:T(8,128)S(1)} %fusion.5) | copy-start | bytes 25165828
